TPU v7x, 32 devices: a whole 2x2x4 slice. The times are simulated.
32 devices in a mesh: freq: 2 (over x), param: 4 (over y, core), sens: 4 (over z).
Axes of the slice: x: 2, y: 2, z: 4, core: 2. Of those that a mesh axis runs over, the one named last changes fastest.
Arguments:
- series: bfloat16 [8, 600, 52], P(None, 'sens', 'freq'), may hold values from -6 to 6
- kernel: bfloat16 [2, 32, 600, 4096], P(None, 'freq', 'sens', 'param'), may hold values from -0.1875 to 0.1875
- prior_spectrum: float32 [32], P('freq'), may hold values from 0.3 to 1.5
- prior_scale: float32 [4096], P('param'), may hold values from 0.5 to 2
Outputs:
- adjoint_map: float32 [52, 8, 4096], P('freq', 'sens', 'param')
All inputs are finite; a program needn't handle non-finite values.
Results may differ from a plain program's by a relative error of at most 0.0047.
Values may be sent and summed in bfloat16 or wider, within the bound.
A program may use at most 64 MiB of HBM per device.

v0:
```python
import math
import jax
import jax.numpy as jnp
from jax import lax
from jax.sharding import PartitionSpec as P

LEN = 840
FB_DEV = 16


def extended(cells, sides, width):
    for axis, dim in sides:
        count = lax.axis_size(axis)
        ends = count - 1
        head = lax.slice_in_dim(cells, 0, width, axis=dim)
        tail = lax.slice_in_dim(cells, cells.shape[dim] - width, cells.shape[dim], axis=dim)
        cells = jnp.concatenate(
            [
                lax.ppermute(tail, axis, [(i, (i + 1) % count) for i in range(ends)]),
                cells,
                lax.ppermute(head, axis, [((i + 1) % count, i) for i in range(ends)]),
            ],
            axis=dim,
        )
    return cells


def phase_tables(bin_first, bin_count, time_count):
    bin_index = bin_first + jnp.arange(bin_count, dtype=jnp.int32)
    time_index = jnp.arange(time_count, dtype=jnp.int32)
    product = time_index[:, None] * bin_index[None, :] % LEN
    phase_angle = product.astype(jnp.float32) * (2.0 * math.pi / LEN)
    return (jnp.cos(phase_angle), jnp.sin(phase_angle))


def contract(spectrum, operator):
    return jnp.einsum("bsr,bsp->brp", spectrum, operator, preferred_element_type=jnp.float32)


def local(series, kernel, prior_spectrum, prior_scale):
    highest = lax.Precision.HIGHEST
    groups = lax.axis_size("freq")
    first_bin = lax.axis_index("freq") * FB_DEV
    probes, sens_dev, time_dev = series.shape
    total_times = time_dev * groups
    cosine, sine_part = phase_tables(first_bin, FB_DEV, total_times)
    phase_table = jnp.concatenate([cosine, -sine_part], axis=1)
    series_piece = lax.all_gather(series, "freq", axis=2, tiled=True)
    row_count = series_piece.shape[2]
    flat_rows = series_piece.astype(jnp.float32).reshape(-1, row_count)
    spectra = jnp.dot(flat_rows, phase_table, precision=highest)
    spectra = (spectra * (1.0 / math.sqrt(total_times))).astype(jnp.bfloat16)
    both_parts = (
        spectra.reshape(probes, sens_dev, 2, FB_DEV)
        .transpose(3, 1, 2, 0)
        .reshape(FB_DEV, sens_dev, 2 * probes)
    )
    with_real = contract(both_parts, kernel[0])
    with_imag = contract(both_parts, kernel[1])
    real_part = with_real[:, :probes] + with_imag[:, probes:]
    imag_part = with_real[:, probes:] - with_imag[:, :probes]
    partial_value = jnp.stack([real_part, imag_part])
    summed = lax.psum_scatter(partial_value, "sens", scatter_dimension=2, tiled=True)
    weights = prior_spectrum * (1.0 / math.sqrt(FB_DEV * groups))
    scaled_spec = summed * weights[None, :, None, None]
    arrived = lax.all_to_all(scaled_spec, "freq", split_axis=3, concat_axis=1, tiled=True)
    bin_total = arrived.shape[1]
    item_count = arrived.shape[2]
    col_count = arrived.shape[3]
    cos_all, sin_all = phase_tables(0, bin_total, total_times)
    full_table = jnp.concatenate([cos_all, -sin_all], axis=1)
    flat_rows = arrived.reshape(2 * bin_total, item_count * col_count)
    arranged = jnp.dot(full_table, flat_rows, precision=highest).reshape(
        total_times, item_count, col_count
    )
    image_field = lax.all_to_all(arranged, "freq", split_axis=0, concat_axis=2, tiled=True)
    weighted = image_field * prior_scale
    padded = extended(weighted, (("param", 2),), 1)
    smooth = 0.5 * weighted + 0.25 * (padded[:, :, :-2] + padded[:, :, 2:])
    return smooth * prior_scale


def solution(mesh):
    placed = (P(None, "sens", "freq"), P(None, "freq", "sens", "param"), P("freq"), P("param"))
    return jax.shard_map(
        local, mesh=mesh, in_specs=placed, out_specs=P("freq", "sens", "param"), check_vma=False
    )
```

profile of v0, /device:TPU:1, one launch (start us, length us, event | category | flops | bytes accessed | tf_op | source)
XLA Modules:
  0.0 111.2 jit_solution(6841817095177923095)
XLA Ops:
  6.5 0.0 reduce-scatter.2.cloned.1.call-start
  6.5 0.1 fusion.32
  6.7 5.6 %all_gather.3 = bf16[8,150,52]{1,0,2:T(8,128)(2,1)S(1)} all-gather(bf16[8,150,26]{1,0,2:T(8,128)(2,1)} %param.4), channel_id=1, replica_groups=mesh['freq'=2,'param'=4,'sens'=4] {'freq'}, dimensions={2}, use_global_device_ids=true | all-gather | bytes 187200 | tf_op jit(solution)/shard_map/all_gather | solution.py:48
  12.3 0.2 reshape.21
  12.5 0.2 fusion.3
  12.8 0.2 reshape.22
  13.0 7.8 %fusion.36 = (bf16[1,16,150,1024]{3,1,2,0:T(8,128)(2,1)S(1)}, bf16[1,16,150,1024]{3,1,2,0:T(8,128)(2,1)}) fusion(bf16[2,16,150,1024]{3,1,2,0:T(8,128)(2,1)} %param.5), kind=kLoop, calls=%fused_computation.55 | loop fusion | bytes 19660800 | tf_op jit(solution)/shard_map/slice | solution.py:58
  20.8 7.8 %fusion = f32[16,16,1024]{2,1,0:T(8,128)S(1)} fusion(bf16[1,16,150,1024]{3,1,2,0:T(8,128)(2,1)} %get-tuple-element.6, bf16[8,150,2,16]{1,0,3,2:T(8,128)(2,1)S(1)} %reshape.22), kind=kOutput, calls=%fused_computation.1 | convolution fusion | flops 78643200 | bytes 6040576 | tf_op jit(solution)/shard_map/bsr,bsp->brp/dot_general | solution.py:37
  28.6 5.6 %fusion.1 = f32[16,16,1024]{2,1,0:T(8,128)S(1)} fusion(bf16[1,16,150,1024]{3,1,2,0:T(8,128)(2,1)S(1)} %get-tuple-element.5, bf16[8,150,2,16]{1,0,3,2:T(8,128)(2,1)S(1)} %reshape.22), kind=kOutput, calls=%fused_computation.3 | convolution fusion | flops 78643200 | bytes 6040576 | tf_op jit(solution)/shard_map/bsr,bsp->brp/dot_general | solution.py:37
  34.2 0.0 copy-start.1
  34.2 0.1 fusion.5
  34.3 0.1 pad_maximum_fusion
  34.4 1.6 %copy.43 = f32[2,16,8,1024]{3,1,0,2:T(8,128)} copy(f32[2,16,8,1024]{3,2,1,0:T(8,128)S(1)} %pad_maximum_fusion) | data formatting | bytes 2097152 | tf_op jit(solution)/shard_map/stack | solution.py:62
  36.0 0.0 reduce-scatter.2.cloned.1.call-update
  36.0 0.0 copy-done.1
  36.0 29.0 %reduce-scatter.2.cloned.1.call-done = f32[2,16,2,1024]{3,1,0,2:T(8,128)} async-done(((f32[2,16,8,1024]{3,1,0,2:T(8,128)}), f32[2,16,2,1024]{3,1,0,2:T(8,128)}) %reduce-scatter.2.cloned.1.call-update) | async-done | bytes 262160 | tf_op jit(solution)/shard_map/reduce_scatter | solution.py:63
  65.1 1.0 broadcast_multiply_fusion
  66.1 1.3 %copy.44 = f32[2,16,2,1024]{1,2,0,3:T(2,128)S(1)} copy(f32[2,16,2,1024]{3,1,0,2:T(8,128)S(1)} %broadcast_multiply_fusion) | data formatting | bytes 524288 | tf_op jit(solution)/shard_map/mul | solution.py:65
  67.5 0.0 copy-start
  67.5 3.6 %reshape.26 = f32[2,1,32768]{2,1,0:T(1,128)} reshape(f32[1024,2,2,16]{3,2,1,0:T(2,128)S(1)} %bitcast.53) | data formatting | bytes 524288
  71.0 3.4 %all-to-all-start = ((f32[2,1,32768]{2,1,0:T(1,128)}), f32[2,1,32768]{2,1,0:T(1,128)S(1)}, u32[]{:S(2)}, u32[]{:S(2)}) async-start(f32[2,1,32768]{2,1,0:T(1,128)} %reshape.26), calls=%async_computation.1 | async-start | bytes 524288 | tf_op jit(solution)/shard_map/all_to_all | solution.py:66
  74.5 0.1 sine_negate_fusion
  74.6 3.9 %all-to-all-done = f32[2,1,32768]{2,1,0:T(1,128)S(1)} async-done(((f32[2,1,32768]{2,1,0:T(1,128)}), f32[2,1,32768]{2,1,0:T(1,128)S(1)}, u32[]{:S(2)}, u32[]{:S(2)}) %all-to-all-start) | async-done | bytes 262176 | tf_op jit(solution)/shard_map/all_to_all | solution.py:66
  78.5 0.5 broadcast.17
  79.0 1.4 %reduce = f32[2,32768]{1,0:T(2,128)S(1)} reduce(f32[2,1,32768]{2,1,0:T(1,128)S(1)} %all-to-all-done, f32[]{:T(128)} %broadcast.17), dimensions={1}, to_apply=%all_to_all.24.reduce_sub_computation | reduce | bytes 524292 | tf_op jit(solution)/shard_map/all_to_all | solution.py:66
  80.5 2.8 %reshape.27 = f32[1024,2,2,16]{3,2,1,0:T(2,128)S(1)} reshape(f32[2,32768]{1,0:T(2,128)S(1)} %reduce) | data formatting | bytes 524288
  83.3 1.5 %copy.45 = f32[2,16,2,2,512]{4,2,1,3,0:T(2,128)S(1)} copy(f32[2,16,2,2,512]{1,2,0,4,3:T(2,128)S(1)} %bitcast.54) | data formatting | bytes 524288 | tf_op jit(solution)/shard_map/all_to_all | solution.py:66
  84.7 0.4 fusion.6
  85.1 0.2 copy.47
  85.3 6.1 %all_to_all.33 = f32[52,2,512]{2,1,0:T(2,128)S(1)} all-to-all(f32[52,2,512]{2,1,0:T(2,128)S(1)} %copy.47), channel_id=1, replica_groups=mesh['freq'=2,'param'=4,'sens'=4] {'freq'}, dimensions={0} | all-to-all | bytes 425984 | tf_op jit(solution)/shard_map/all_to_all | solution.py:76
  91.4 0.0 copy-done
  91.5 0.1 broadcast_multiply_fusion.1
  91.5 0.1 fusion.37
  91.6 6.4 %collective-permute-start = (f32[26,2,1]{2,1,0:T(2,128)S(1)}, f32[26,2,1]{2,1,0:T(2,128)S(1)}, u32[]{:S(2)}, u32[]{:S(2)}) collective-permute-start(f32[26,2,1]{2,1,0:T(2,128)S(1)} %get-tuple-element.9), channel_id=1, source_target_pairs={{0,4},{4,8},{8,12},{1,5},{5,9},{9,13},{2,6},{6,10},{10,14},{3,7},{... | collective-permute-start | bytes 632 | tf_op jit(solution)/shard_map/ppermute | solution.py:19
  98.0 1.9 %collective-permute-start.1 = (f32[26,2,1]{2,1,0:T(2,128)S(1)}, f32[26,2,1]{2,1,0:T(2,128)S(1)}, u32[]{:S(2)}, u32[]{:S(2)}) collective-permute-start(f32[26,2,1]{2,1,0:T(2,128)S(1)} %get-tuple-element.10), channel_id=1, source_target_pairs={{4,0},{8,4},{12,8},{5,1},{9,5},{13,9},{6,2},{10,6},{14,10},{7,3},{... | collective-permute-start | bytes 632 | tf_op jit(solution)/shard_map/ppermute | solution.py:21
  99.9 0.0 collective-permute-done
  99.9 3.2 %collective-permute-done.1 = f32[26,2,1]{2,1,0:T(2,128)S(1)} collective-permute-done((f32[26,2,1]{2,1,0:T(2,128)S(1)}, f32[26,2,1]{2,1,0:T(2,128)S(1)}, u32[]{:S(2)}, u32[]{:S(2)}) %collective-permute-start.1) | collective-permute-done | bytes 240 | tf_op jit(solution)/shard_map/ppermute | solution.py:21
  103.2 1.2 %fusion.12 = f32[26,2,1024]{2,1,0:T(2,128)} fusion(f32[26,2,1]{2,1,0:T(2,128)S(1)} %collective-permute-done.1, f32[26,2,1024]{2,1,0:T(2,128)S(1)} %broadcast_multiply_fusion.1, f32[26,2,1]{2,1,0:T(2,128)S(1)} %collective-permute-done, f32[1024]{0:T(1024)S(1)} %copy-done), kind=kLoop, calls=%fused_computation.20 | loop fusion | flops 372736 | bytes 430496 | tf_op jit(solution)/shard_map/mul | solution.py:80
  (3 shorter events, 0.0 us)
Async XLA Ops:
  6.5 58.5 %reduce-scatter.2.cloned.1.call-start = ((), (), s32[]{:S(2)}) async-start(), calls=%async_computation.3 | async-start | bytes 1310720 | tf_op jit(solution)/shard_map/reduce_scatter | solution.py:63
  34.2 1.8 %copy-start.1 = (f32[16]{0:T(128)S(1)}, f32[16]{0:T(128)}, u32[]{:S(2)}) copy-start(f32[16]{0:T(128)} %param.6) | copy-start | bytes 196
  67.5 24.0 %copy-start = (f32[1024]{0:T(1024)S(1)}, f32[1024]{0:T(1024)}, u32[]{:S(2)}) copy-start(f32[1024]{0:T(1024)} %param.7) | copy-start | bytes 12292
  71.0 7.5 %all-to-all-start = ((f32[2,1,32768]{2,1,0:T(1,128)}), f32[2,1,32768]{2,1,0:T(1,128)S(1)}, u32[]{:S(2)}, u32[]{:S(2)}) async-start(f32[2,1,32768]{2,1,0:T(1,128)} %reshape.26), calls=%async_computation.1 | async-start | bytes 524288 | tf_op jit(solution)/shard_map/all_to_all | solution.py:66
  91.6 8.3 %collective-permute-start = (f32[26,2,1]{2,1,0:T(2,128)S(1)}, f32[26,2,1]{2,1,0:T(2,128)S(1)}, u32[]{:S(2)}, u32[]{:S(2)}) collective-permute-start(f32[26,2,1]{2,1,0:T(2,128)S(1)} %get-tuple-element.9), channel_id=1, source_target_pairs={{0,4},{4,8},{8,12},{1,5},{5,9},{9,13},{2,6},{6,10},{10,14},{3,7},{... | collective-permute-start | bytes 632 | tf_op jit(solution)/shard_map/ppermute | solution.py:19
  98.0 5.2 %collective-permute-start.1 = (f32[26,2,1]{2,1,0:T(2,128)S(1)}, f32[26,2,1]{2,1,0:T(2,128)S(1)}, u32[]{:S(2)}, u32[]{:S(2)}) collective-permute-start(f32[26,2,1]{2,1,0:T(2,128)S(1)} %get-tuple-element.10), channel_id=1, source_target_pairs={{4,0},{8,4},{12,8},{5,1},{9,5},{13,9},{6,2},{10,6},{14,10},{7,3},{... | collective-permute-start | bytes 632 | tf_op jit(solution)/shard_map/ppermute | solution.py:21
Sparse Core Ops, SparseCore 0:
  36.1 28.8 reduce-scatter.1
where the time goes:
time: 112 us; the launch traced here: 111 us
  waiting for transfers between devices  36.2 us (32%)
  local copies, waits for them, and re-layouts  19.8 us (18%)
  matrix products  14 us (12%)
  between operations  13.6 us (12%)
  starting transfers between devices  11.7 us (10%)
  blocking collectives  11.7 us (10%)
  other arithmetic  4.27 us (4%)
    reduce_scatter x1, waiting for transfers between devices, local(): lax.psum_scatter(partial_value, 'sens', scatter_dimension=2, tiled=True)  29 us
    dot_general x2, matrix products, contract(): jnp.einsum('bsr,bsp->brp', spectrum, operator, preferred_element_type=jnp...  13.4 us
    slice x1, local copies, waits for them, and re-layouts, local(): with_real = contract(both_parts, kernel[0])  7.77 us
    unnamed x6, local copies, waits for them, and re-layouts  6.39 us
    ppermute x1, starting transfers between devices, extended(): lax.ppermute(tail, axis, [(i, (i + 1) % count) for i in range(ends)])  6.36 us
    all_to_all x1, blocking collectives, local(): lax.all_to_all(arranged, 'freq', split_axis=0, concat_axis=2, tiled=True)  6.12 us
    all_gather x1, blocking collectives, local(): series_piece = lax.all_gather(series, 'freq', axis=2, tiled=True)  5.63 us
    all_to_all x1, waiting for transfers between devices, local(): lax.all_to_all(scaled_spec, 'freq', split_axis=3, concat_axis=1, tiled=True)  3.86 us
  transfers between devices with their start and end apart: 4, of which 3 were waited for; matrix products, arithmetic and copies ran while one was open for 0% of the time, Pallas kernels for 0%

commit v1 on v0

--- a/solution.py
+++ b/solution.py
@@ -63,7 +63,10 @@
     summed = lax.psum_scatter(partial_value, "sens", scatter_dimension=2, tiled=True)
     weights = prior_spectrum * (1.0 / math.sqrt(FB_DEV * groups))
     scaled_spec = summed * weights[None, :, None, None]
-    arrived = lax.all_to_all(scaled_spec, "freq", split_axis=3, concat_axis=1, tiled=True)
+    size = lax.axis_size("freq")
+    parts = jnp.stack(jnp.split(scaled_spec, size, axis=3), axis=0)
+    parts = lax.all_to_all(parts, "freq", split_axis=0, concat_axis=0)
+    arrived = jnp.concatenate(parts, axis=1)
     bin_total = arrived.shape[1]
     item_count = arrived.shape[2]
     col_count = arrived.shape[3]

time: 112 us -> 101 us (0.902)
  local copies, waits for them, and re-layouts: 19.8 us -> 10.3 us
    unnamed x6 -> x4, local copies, waits for them, and re-layouts: 6.39 us -> 0.01 us
    all_to_all x2 -> x0, local copies, waits for them, and re-layouts: 1.96 us -> none  [local(): lax.all_to_all(scaled_spec, 'freq', split_axis=3, concat_axis=1, tiled=True)]
    all_to_all x1 -> x0, other arithmetic: 1.44 us -> none  [local(): lax.all_to_all(scaled_spec, 'freq', split_axis=3, concat_axis=1, tiled=True)]
    mul x1 -> x0, local copies, waits for them, and re-layouts: 1.35 us -> none  [local(): scaled_spec = summed * weights[None, :, None, None]]
where the time goes in v1:
time: 101 us
  waiting for transfers between devices  36.2 us (36%)
  matrix products  14 us (14%)
  between operations  13.5 us (13%)
  starting transfers between devices  11.7 us (12%)
  blocking collectives  11.7 us (12%)
  local copies, waits for them, and re-layouts  10.3 us (10%)
  other arithmetic  3.55 us (4%)
    reduce_scatter x1, waiting for transfers between devices, local(): lax.psum_scatter(partial_value, 'sens', scatter_dimension=2, tiled=True)  29 us
    dot_general x2, matrix products, contract(): jnp.einsum('bsr,bsp->brp', spectrum, operator, preferred_element_type=jnp...  13.4 us
    slice x1, local copies, waits for them, and re-layouts, local(): with_real = contract(both_parts, kernel[0])  7.79 us
    ppermute x1, starting transfers between devices, extended(): lax.ppermute(tail, axis, [(i, (i + 1) % count) for i in range(ends)])  6.35 us
    all_to_all x1, blocking collectives, local(): lax.all_to_all(arranged, 'freq', split_axis=0, concat_axis=2, tiled=True)  6.12 us
    all_gather x1, blocking collectives, local(): series_piece = lax.all_gather(series, 'freq', axis=2, tiled=True)  5.63 us
    all_to_all x1, waiting for transfers between devices, local(): parts = lax.all_to_all(parts, 'freq', split_axis=0, concat_axis=0)  3.86 us
    all_to_all x1, starting transfers between devices, local(): parts = lax.all_to_all(parts, 'freq', split_axis=0, concat_axis=0)  3.44 us
  transfers between devices with their start and end apart: 4, of which 3 were waited for; matrix products, arithmetic and copies ran while one was open for 0% of the time, Pallas kernels for 0%

profile of v1, /device:TPU:1, one launch (start us, length us, event | category | flops | bytes accessed | tf_op | source)
XLA Modules:
  0.0 101.1 jit_solution(10629813969651405531)
XLA Ops:
  6.5 0.0 reduce-scatter.2.cloned.1.call-start
  6.5 0.1 fusion.32
  6.7 5.6 %all_gather.3 = bf16[8,150,52]{1,0,2:T(8,128)(2,1)S(1)} all-gather(bf16[8,150,26]{1,0,2:T(8,128)(2,1)} %param.4), channel_id=1, replica_groups=mesh['freq'=2,'param'=4,'sens'=4] {'freq'}, dimensions={2}, use_global_device_ids=true | all-gather | bytes 187200 | tf_op jit(solution)/shard_map/all_gather | solution.py:48
  12.3 0.2 reshape.20
  12.5 0.2 fusion.3
  12.8 0.2 reshape.21
  13.0 7.8 %fusion.36 = (bf16[1,16,150,1024]{3,1,2,0:T(8,128)(2,1)S(1)}, bf16[1,16,150,1024]{3,1,2,0:T(8,128)(2,1)}) fusion(bf16[2,16,150,1024]{3,1,2,0:T(8,128)(2,1)} %param.5), kind=kLoop, calls=%fused_computation.58 | loop fusion | bytes 19660800 | tf_op jit(solution)/shard_map/slice | solution.py:58
  20.8 7.8 %fusion = f32[16,16,1024]{2,1,0:T(8,128)S(1)} fusion(bf16[1,16,150,1024]{3,1,2,0:T(8,128)(2,1)} %get-tuple-element.6, bf16[8,150,2,16]{1,0,3,2:T(8,128)(2,1)S(1)} %reshape.21), kind=kOutput, calls=%fused_computation.1 | convolution fusion | flops 78643200 | bytes 6040576 | tf_op jit(solution)/shard_map/bsr,bsp->brp/dot_general | solution.py:37
  28.6 5.6 %fusion.1 = f32[16,16,1024]{2,1,0:T(8,128)S(1)} fusion(bf16[1,16,150,1024]{3,1,2,0:T(8,128)(2,1)S(1)} %get-tuple-element.5, bf16[8,150,2,16]{1,0,3,2:T(8,128)(2,1)S(1)} %reshape.21), kind=kOutput, calls=%fused_computation.3 | convolution fusion | flops 78643200 | bytes 6040576 | tf_op jit(solution)/shard_map/bsr,bsp->brp/dot_general | solution.py:37
  34.2 0.0 copy-start.1
  34.2 0.1 fusion.5
  34.3 0.0 copy-start
  34.3 0.1 pad_maximum_fusion
  34.4 1.6 %copy.33 = f32[2,16,8,1024]{3,1,0,2:T(8,128)} copy(f32[2,16,8,1024]{3,2,1,0:T(8,128)S(1)} %pad_maximum_fusion) | data formatting | bytes 2097152 | tf_op jit(solution)/shard_map/stack | solution.py:62
  36.0 0.0 reduce-scatter.2.cloned.1.call-update
  36.0 0.0 copy-done.1
  36.1 29.0 %reduce-scatter.2.cloned.1.call-done = f32[2,16,2,1024]{3,1,0,2:T(8,128)} async-done(((f32[2,16,8,1024]{3,1,0,2:T(8,128)}), f32[2,16,2,1024]{3,1,0,2:T(8,128)}) %reduce-scatter.2.cloned.1.call-update) | async-done | bytes 262160 | tf_op jit(solution)/shard_map/reduce_scatter | solution.py:63
  65.1 1.0 %broadcast_multiply_fusion = f32[2,16,2,1024]{3,1,0,2:T(8,128)S(1)} fusion(f32[2,16,2,1024]{3,1,0,2:T(8,128)} %reduce-scatter.2.cloned.1.call-done, f32[16]{0:T(128)S(1)} %broadcast_multiply_fusion.2), kind=kLoop, calls=%fused_computation.26 | loop fusion | flops 65536 | bytes 524352 | tf_op jit(solution)/shard_map/mul | solution.py:65
  66.2 0.7 pad_maximum_fusion.1
  66.9 3.4 %all-to-all-start = ((f32[2,2,16,2,512]{4,2,1,3,0:T(8,128)}), f32[2,2,16,2,512]{4,2,1,3,0:T(8,128)S(1)}, u32[]{:S(2)}, u32[]{:S(2)}) async-start(f32[2,2,16,2,512]{4,2,1,3,0:T(8,128)} %pad_maximum_fusion.1), calls=%async_computation.1 | async-start | bytes 524288 | tf_op jit(solution)/shard_map/all_to_all | solution.py:68
  70.3 0.1 sine_negate_fusion
  70.5 3.9 %all-to-all-done = f32[2,2,16,2,512]{4,2,1,3,0:T(8,128)S(1)} async-done(((f32[2,2,16,2,512]{4,2,1,3,0:T(8,128)}), f32[2,2,16,2,512]{4,2,1,3,0:T(8,128)S(1)}, u32[]{:S(2)}, u32[]{:S(2)}) %all-to-all-start) | async-done | bytes 262176 | tf_op jit(solution)/shard_map/all_to_all | solution.py:68
  74.3 0.2 copy.34
  74.6 0.4 fusion.6
  75.0 0.2 copy.36
  75.1 6.1 %all_to_all.23 = f32[52,2,512]{2,1,0:T(2,128)S(1)} all-to-all(f32[52,2,512]{2,1,0:T(2,128)S(1)} %copy.36), channel_id=1, replica_groups=mesh['freq'=2,'param'=4,'sens'=4] {'freq'}, dimensions={0} | all-to-all | bytes 425984 | tf_op jit(solution)/shard_map/all_to_all | solution.py:79
  81.3 0.0 copy-done
  81.3 0.1 broadcast_multiply_fusion.1
  81.4 0.1 fusion.37
  81.5 6.4 %collective-permute-start = (f32[26,2,1]{2,1,0:T(2,128)S(1)}, f32[26,2,1]{2,1,0:T(2,128)S(1)}, u32[]{:S(2)}, u32[]{:S(2)}) collective-permute-start(f32[26,2,1]{2,1,0:T(2,128)S(1)} %get-tuple-element.11), channel_id=1, source_target_pairs={{0,4},{4,8},{8,12},{1,5},{5,9},{9,13},{2,6},{6,10},{10,14},{3,7},{... | collective-permute-start | bytes 632 | tf_op jit(solution)/shard_map/ppermute | solution.py:19
  87.8 1.9 %collective-permute-start.1 = (f32[26,2,1]{2,1,0:T(2,128)S(1)}, f32[26,2,1]{2,1,0:T(2,128)S(1)}, u32[]{:S(2)}, u32[]{:S(2)}) collective-permute-start(f32[26,2,1]{2,1,0:T(2,128)S(1)} %get-tuple-element.12), channel_id=1, source_target_pairs={{4,0},{8,4},{12,8},{5,1},{9,5},{13,9},{6,2},{10,6},{14,10},{7,3},{... | collective-permute-start | bytes 632 | tf_op jit(solution)/shard_map/ppermute | solution.py:21
  89.7 0.0 collective-permute-done
  89.8 3.2 %collective-permute-done.1 = f32[26,2,1]{2,1,0:T(2,128)S(1)} collective-permute-done((f32[26,2,1]{2,1,0:T(2,128)S(1)}, f32[26,2,1]{2,1,0:T(2,128)S(1)}, u32[]{:S(2)}, u32[]{:S(2)}) %collective-permute-start.1) | collective-permute-done | bytes 240 | tf_op jit(solution)/shard_map/ppermute | solution.py:21
  93.0 1.2 %fusion.12 = f32[26,2,1024]{2,1,0:T(2,128)} fusion(f32[26,2,1]{2,1,0:T(2,128)S(1)} %collective-permute-done.1, f32[26,2,1024]{2,1,0:T(2,128)S(1)} %broadcast_multiply_fusion.1, f32[26,2,1]{2,1,0:T(2,128)S(1)} %collective-permute-done, f32[1024]{0:T(1024)S(1)} %copy-done), kind=kLoop, calls=%fused_computation.21 | loop fusion | flops 372736 | bytes 430496 | tf_op jit(solution)/shard_map/mul | solution.py:83
  (4 shorter events, 0.0 us)
Async XLA Ops:
  6.5 58.6 %reduce-scatter.2.cloned.1.call-start = ((), (), s32[]{:S(2)}) async-start(), calls=%async_computation.3 | async-start | bytes 1310720 | tf_op jit(solution)/shard_map/reduce_scatter | solution.py:63
  34.2 1.9 %copy-start.1 = (f32[16]{0:T(128)S(1)}, f32[16]{0:T(128)}, u32[]{:S(2)}) copy-start(f32[16]{0:T(128)} %param.6) | copy-start | bytes 196
  34.3 46.9 %copy-start = (f32[1024]{0:T(1024)S(1)}, f32[1024]{0:T(1024)}, u32[]{:S(2)}) copy-start(f32[1024]{0:T(1024)} %param.7) | copy-start | bytes 12292
  66.9 7.5 %all-to-all-start = ((f32[2,2,16,2,512]{4,2,1,3,0:T(8,128)}), f32[2,2,16,2,512]{4,2,1,3,0:T(8,128)S(1)}, u32[]{:S(2)}, u32[]{:S(2)}) async-start(f32[2,2,16,2,512]{4,2,1,3,0:T(8,128)} %pad_maximum_fusion.1), calls=%async_computation.1 | async-start | bytes 524288 | tf_op jit(solution)/shard_map/all_to_all | solution.py:68
  81.5 8.3 %collective-permute-start = (f32[26,2,1]{2,1,0:T(2,128)S(1)}, f32[26,2,1]{2,1,0:T(2,128)S(1)}, u32[]{:S(2)}, u32[]{:S(2)}) collective-permute-start(f32[26,2,1]{2,1,0:T(2,128)S(1)} %get-tuple-element.11), channel_id=1, source_target_pairs={{0,4},{4,8},{8,12},{1,5},{5,9},{9,13},{2,6},{6,10},{10,14},{3,7},{... | collective-permute-start | bytes 632 | tf_op jit(solution)/shard_map/ppermute | solution.py:19
  87.8 5.2 %collective-permute-start.1 = (f32[26,2,1]{2,1,0:T(2,128)S(1)}, f32[26,2,1]{2,1,0:T(2,128)S(1)}, u32[]{:S(2)}, u32[]{:S(2)}) collective-permute-start(f32[26,2,1]{2,1,0:T(2,128)S(1)} %get-tuple-element.12), channel_id=1, source_target_pairs={{4,0},{8,4},{12,8},{5,1},{9,5},{13,9},{6,2},{10,6},{14,10},{7,3},{... | collective-permute-start | bytes 632 | tf_op jit(solution)/shard_map/ppermute | solution.py:21
Sparse Core Ops, SparseCore 0:
  36.2 28.8 reduce-scatter.1
